TPU v7x, 32 devices: a whole 2x2x4 slice. The times are simulated.
32 devices in a mesh: dp: 4 (over y, core), tensor: 8 (over z, x).
Axes of the slice: x: 2, y: 2, z: 4, core: 2. Of those that a mesh axis runs over, the one named last changes fastest.
Arguments:
- hidden_in: bfloat16 [512, 8192], P('dp'), may hold values from -20 to 20
- norm_gain: bfloat16 [8192], replicated, may hold values from 0.25 to 1.75
- q_weight: bfloat16 [8192, 8192], P(None, 'tensor'), as said below
- q_grad: bfloat16 [512, 8192], P('dp', 'tensor'), may hold values from -6 to 6
- q_main: float32 [8192, 8192], P('dp', 'tensor'), may hold values from -6 to 6
- weight_main_gradient: float32 [8192], P('tensor'), may hold values from -6 to 6
Outputs:
- hidden_state_gradient: bfloat16 [512, 8192], P('dp', 'tensor')
- q_main_new: float32 [8192, 8192], P('dp', 'tensor')
- weight_main_updated: float32 [8192], P('tensor')
Inputs may be any that keep to these rules, and one draw needn't show every extreme that they name: `q_weight`: entries of mean 0 and deviation about 8192 ** -0.5.
All inputs are finite; a program needn't handle non-finite values.
Results may differ from a plain program's by a relative error of at most 0.03.
Values may be sent and summed in bfloat16 or wider, within the bound.
A program may use at most 128 MiB of HBM per device.

v0:
```python
import jax
import jax.numpy as jnp
from jax import lax
from jax.sharding import PartitionSpec as P


def body(hidden_in, norm_gain, q_weight, q_grad, q_main, weight_main_gradient):
    hidden_state = hidden_in.astype(jnp.float32)
    inverse_root_mean = lax.rsqrt(
        jnp.mean(hidden_state * hidden_state, axis=-1, keepdims=True) + 1e-05
    )
    normalized_rows = hidden_state * inverse_root_mean
    norm_weight = norm_gain.astype(jnp.float32)
    normalized_input = (normalized_rows * norm_weight).astype(jnp.bfloat16)
    hidden_width = q_weight.shape[1]
    ndp = lax.axis_size("dp")
    owner_start = lax.axis_index("tensor") * hidden_width
    partial_value = lax.dot_general(
        q_grad, q_weight, (((1,), (1,)), ((), ())), preferred_element_type=jnp.float32
    )
    owned_normalized_rows = lax.dynamic_slice_in_dim(normalized_rows, owner_start, hidden_width, 1)
    owned_norm_weight = lax.dynamic_slice_in_dim(norm_weight, owner_start, hidden_width, 0)
    reduced_sum = lax.psum(partial_value.astype(jnp.bfloat16), "tensor").astype(jnp.float32)
    row_statistic = jnp.mean(reduced_sum * norm_weight * normalized_rows, axis=-1, keepdims=True)
    owned_gradient = lax.dynamic_slice_in_dim(reduced_sum, owner_start, hidden_width, 1)
    hidden_state_gradient = (
        inverse_root_mean
        * (owned_gradient * owned_norm_weight - owned_normalized_rows * row_statistic)
    ).astype(jnp.bfloat16)
    weight_contribution = jnp.sum(owned_gradient * owned_normalized_rows, axis=0)
    weight_main_updated = weight_main_gradient + lax.psum(weight_contribution, "dp") / ndp
    product = lax.dot_general(
        normalized_input, q_grad, (((0,), (0,)), ((), ())), preferred_element_type=jnp.float32
    )
    q_main_new = q_main + lax.psum_scatter(
        (product / ndp).astype(jnp.bfloat16), "dp", scatter_dimension=0, tiled=True
    ).astype(jnp.float32)
    return (hidden_state_gradient, q_main_new, weight_main_updated)


def solution(mesh):
    in_specs = (
        P("dp", None),
        P(),
        P(None, "tensor"),
        P("dp", "tensor"),
        P("dp", "tensor"),
        P("tensor"),
    )
    out_specs = (P("dp", "tensor"), P("dp", "tensor"), P("tensor"))
    return jax.shard_map(body, mesh=mesh, in_specs=in_specs, out_specs=out_specs, check_vma=False)
```

profile of v0, /device:TPU:0, one launch (start us, length us, event | category | flops | bytes accessed | tf_op | source)
XLA Modules:
  0.0 176.3 jit_solution(3481527739017991121)
XLA Ops:
  8.0 0.0 copy-start
  8.0 0.0 copy-start.4
  8.0 0.0 copy-start.3
  8.0 0.0 all-reduce.2.cloned.1.call-start
  8.1 0.9 copy-done
  9.0 12.7 %convolution_convert_fusion = bf16[128,8192]{1,0:T(8,128)(2,1)} fusion(bf16[128,1024]{1,0:T(8,128)(2,1)S(1)} %copy-done, bf16[8192,1024]{1,0:T(8,128)(2,1)} %param.8), kind=kOutput, calls=%fused_computation.1 | convolution fusion | flops 2148532224 | bytes 19136512 | tf_op jit(solution)/shard_map/dot_general | solution.py:18
  21.7 0.0 all-reduce.2.cloned.1.call-update
  21.7 0.0 reduce-scatter.2.cloned.1.call-start
  21.7 0.0 copy-done.4
  21.8 0.0 copy-done.3
  21.8 0.5 fusion
  22.3 8.5 %multiply_convert_fusion = bf16[8192,1024]{1,0:T(8,128)(2,1)} fusion(bf16[128,1024]{1,0:T(8,128)(2,1)S(1)} %copy-done, f32[8192]{0:T(1024)S(1)} %convert_element_type.27, bf16[128,8192]{1,0:T(8,128)(2,1)S(1)} %copy-done.3, f32[128]{0:T(128)S(1)} %add_rsqrt_fusion), kind=kOutput, calls=%fused_computation | convolution fusion | flops 2168455168 | bytes 19169792 | tf_op jit(solution)/shard_map/dot_general | solution.py:32
  30.7 0.0 reduce-scatter.2.cloned.1.call-update
  30.8 96.1 %all-reduce.2.cloned.1.call-done = bf16[128,8192]{1,0:T(8,128)(2,1)} async-done(((bf16[128,8192]{1,0:T(8,128)(2,1)}), bf16[128,8192]{1,0:T(8,128)(2,1)}) %all-reduce.2.cloned.1.call-update) | async-done | bytes 2097168 | tf_op jit(solution)/shard_map/psum | solution.py:23
  126.9 0.0 copy-start.2
  126.9 2.1 %convert_element_type.26 = f32[128,8192]{1,0:T(8,128)S(1)} convert(bf16[128,8192]{1,0:T(8,128)(2,1)} %all-reduce.2.cloned.1.call-done) | non-fusion elementwise | flops 1048576 | bytes 6291456 | tf_op jit(solution)/shard_map/convert_element_type | solution.py:23
  129.0 0.1 copy-done.2
  129.1 0.0 copy-start.5
  129.1 1.3 multiply_reduce_fusion
  130.4 0.9 multiply_reduce_fusion.1
  131.2 6.9 %psum.15 = f32[1024]{0:T(1024)S(1)} all-reduce(f32[1024]{0:T(1024)S(1)} %get-tuple-element.3), channel_id=1, replica_groups=mesh['dp'=4,'tensor'=8] {'dp'}, use_global_device_ids=true, to_apply=%region_5.0 | all-reduce | flops 1024 | bytes 8192 | tf_op jit(solution)/shard_map/psum | solution.py:31
  138.2 0.0 copy-done.5
  138.2 0.6 multiply_add_fusion
  138.8 19.8 %reduce-scatter.2.cloned.1.call-done = bf16[2048,1024]{1,0:T(8,128)(2,1)} async-done(((bf16[8192,1024]{1,0:T(8,128)(2,1)}), bf16[2048,1024]{1,0:T(8,128)(2,1)}) %reduce-scatter.2.cloned.1.call-update) | async-done | bytes 4194320 | tf_op jit(solution)/shard_map/reduce_scatter | solution.py:35
  158.6 0.0 copy-start.1
  158.6 10.2 %convert_add_fusion = f32[2048,1024]{1,0:T(8,128)} fusion(f32[2048,1024]{1,0:T(8,128)} %param.10, bf16[2048,1024]{1,0:T(8,128)(2,1)} %reduce-scatter.2.cloned.1.call-done), kind=kLoop, calls=%fused_computation.2 | loop fusion | flops 4194304 | bytes 20971520 | tf_op jit(solution)/shard_map/add | solution.py:35
  168.8 0.0 copy-done.1
  (4 shorter events, 0.0 us)
Async XLA Ops:
  8.0 1.0 copy-start
  8.0 13.7 %copy-start.4 = (bf16[8192]{0:T(1024)(128)(2,1)S(1)}, bf16[8192]{0:T(1024)(128)(2,1)}, u32[]{:S(2)}) copy-start(bf16[8192]{0:T(1024)(128)(2,1)} %param.7) | copy-start | bytes 49156
  8.0 13.7 %copy-start.3 = (bf16[128,8192]{1,0:T(8,128)(2,1)S(1)}, bf16[128,8192]{1,0:T(8,128)(2,1)}, u32[]{:S(2)}) copy-start(bf16[128,8192]{1,0:T(8,128)(2,1)} %param.6) | copy-start | bytes 6291460
  8.0 118.8 %all-reduce.2.cloned.1.call-start = ((), (), s32[]{:S(2)}) async-start(), calls=%async_computation.1 | async-start | bytes 4194304 | tf_op jit(solution)/shard_map/psum | solution.py:23
  21.7 136.9 %reduce-scatter.2.cloned.1.call-start = ((), (), s32[]{:S(2)}) async-start(), calls=%async_computation.2 | async-start | bytes 20971520 | tf_op jit(solution)/shard_map/reduce_scatter | solution.py:35
  126.9 2.2 %copy-start.2 = (bf16[128,8192]{1,0:T(8,128)(2,1)S(1)}, bf16[128,8192]{1,0:T(8,128)(2,1)}, u32[]{:S(2)}) copy-start(bf16[128,8192]{1,0:T(8,128)(2,1)} %all-reduce.2.cloned.1.call-done) | copy-start | bytes 6291460
  129.1 9.1 %copy-start.5 = (f32[1024]{0:T(1024)S(1)}, f32[1024]{0:T(1024)}, u32[]{:S(2)}) copy-start(f32[1024]{0:T(1024)} %param.11) | copy-start | bytes 12292
  158.6 10.2 %copy-start.1 = (bf16[128,1024]{1,0:T(8,128)(2,1)S(1)}, bf16[128,1024]{1,0:T(8,128)(2,1)}, u32[]{:S(2)}) copy-start(bf16[128,1024]{1,0:T(8,128)(2,1)} %param.9) | copy-start | bytes 786436
Sparse Core Ops, SparseCore 0:
  21.8 105.0 all-reduce.1
Sparse Core Ops, SparseCore 1:
  30.9 127.7 reduce-scatter.1
where the time goes:
time: 176 us
  waiting for transfers between devices  116 us (66%)
  matrix products  21.2 us (12%)
  other arithmetic  15.6 us (9%)
  between operations  15.6 us (9%)
  blocking collectives  6.94 us (4%)
    psum x1, waiting for transfers between devices, body(): lax.psum(partial_value.astype(jnp.bfloat16), 'tensor').astype(jnp.float32)  96.1 us
    reduce_scatter x1, waiting for transfers between devices, body(): lax.psum_scatter((product / ndp).astype(jnp.bfloat16), 'dp', scatter_dime...  19.8 us
    dot_general x1, matrix products, body(): lax.dot_general(q_grad, q_weight, (((1,), (1,)), ((), ())), preferred_ele...  12.7 us
    add x1, other arithmetic, body(): q_main + lax.psum_scatter((product / ndp).astype(jnp.bfloat16), 'dp', sca...  10.2 us
    dot_general x1, matrix products, body(): lax.dot_general(normalized_input, q_grad, (((0,), (0,)), ((), ())), prefe...  8.48 us
    psum x1, blocking collectives, body(): lax.psum(weight_contribution, 'dp') / ndp  6.94 us
  transfers between devices with their start and end apart: 2, of which 2 were waited for; matrix products, arithmetic and copies ran while one was open for 8% of the time, Pallas kernels for 0%

commit v1 on v0

--- a/solution.py
+++ b/solution.py
@@ -20,7 +20,9 @@
     )
     owned_normalized_rows = lax.dynamic_slice_in_dim(normalized_rows, owner_start, hidden_width, 1)
     owned_norm_weight = lax.dynamic_slice_in_dim(norm_weight, owner_start, hidden_width, 0)
-    reduced_sum = lax.psum(partial_value.astype(jnp.bfloat16), "tensor").astype(jnp.float32)
+    reduced_sum = jnp.sum(
+        lax.all_gather(partial_value.astype(jnp.bfloat16), "tensor"), axis=0
+    ).astype(jnp.float32)
     row_statistic = jnp.mean(reduced_sum * norm_weight * normalized_rows, axis=-1, keepdims=True)
     owned_gradient = lax.dynamic_slice_in_dim(reduced_sum, owner_start, hidden_width, 1)
     hidden_state_gradient = (

time: 176 us -> 289 us (1.64)
  waiting for transfers between devices: 116 us -> 221 us
  other arithmetic: 15.6 us -> 23 us
    all_gather x0 -> x1, waiting for transfers between devices: none -> 221 us  [body(): lax.all_gather(partial_value.astype(jnp.bfloat16), 'tensor')]
    psum x1 -> x0, waiting for transfers between devices: 96.1 us -> none  [body(): lax.psum(partial_value.astype(jnp.bfloat16), 'tensor').astype(jnp.float32)]
    reduce_scatter x1, waiting for transfers between devices: 19.8 us -> 0.01 us  [body(): lax.psum_scatter((product / ndp).astype(jnp.bfloat16), 'dp', scatter_dime...]
    reduce_sum x0 -> x1, other arithmetic: none -> 9.14 us  [body(): jnp.sum(lax.all_gather(partial_value.astype(jnp.bfloat16), 'tensor'), axi...]
  transfers between devices with their start and end apart: 2 -> 2, of which waited for: 2 -> 1; matrix products, arithmetic and copies ran while one was open for 8% -> 7% of each run, Pallas kernels for 0% -> 0%
where the time goes in v1:
time: 289 us
  waiting for transfers between devices  221 us (76%)
  other arithmetic  23 us (8%)
  matrix products  20.9 us (7%)
  between operations  15.6 us (5%)
  blocking collectives  5.82 us (2%)
    all_gather x1, waiting for transfers between devices, body(): lax.all_gather(partial_value.astype(jnp.bfloat16), 'tensor')  221 us
    dot_general x1, matrix products, body(): lax.dot_general(q_grad, q_weight, (((1,), (1,)), ((), ())), preferred_ele...  12.7 us
    add x1, other arithmetic, body(): q_main + lax.psum_scatter((product / ndp).astype(jnp.bfloat16), 'dp', sca...  10.2 us
    reduce_sum x1, other arithmetic, body(): jnp.sum(lax.all_gather(partial_value.astype(jnp.bfloat16), 'tensor'), axi...  9.14 us
    dot_general x1, matrix products, body(): lax.dot_general(normalized_input, q_grad, (((0,), (0,)), ((), ())), prefe...  8.22 us
    psum x1, blocking collectives, body(): lax.psum(weight_contribution, 'dp') / ndp  5.82 us
  transfers between devices with their start and end apart: 2, of which 1 were waited for; matrix products, arithmetic and copies ran while one was open for 7% of the time, Pallas kernels for 0%

profile of v1, /device:TPU:0, one launch (start us, length us, event | category | flops | bytes accessed | tf_op | source)
XLA Modules:
  0.0 288.8 jit_solution(17490629362064678059)
XLA Ops:
  8.0 0.0 copy-start
  8.0 0.0 copy-start.4
  8.0 0.0 copy-start.2
  8.0 0.0 all-gather.3.cloned.1.call-start
  8.1 0.9 copy-done
  9.0 12.7 %convolution_convert_fusion = bf16[128,8192]{1,0:T(8,128)(2,1)} fusion(bf16[128,1024]{1,0:T(8,128)(2,1)S(1)} %copy-done, bf16[8192,1024]{1,0:T(8,128)(2,1)} %param.8), kind=kOutput, calls=%fused_computation.1 | convolution fusion | flops 2148532224 | bytes 19136512 | tf_op jit(solution)/shard_map/dot_general | solution.py:18
  21.7 0.0 all-gather.3.cloned.1.call-update
  21.7 0.0 reduce-scatter.2.cloned.1.call-start
  21.7 0.0 copy-done.4
  21.8 0.0 copy-done.2
  21.8 0.5 fusion
  22.3 8.2 %multiply_convert_fusion = bf16[8192,1024]{1,0:T(8,128)(2,1)} fusion(bf16[128,1024]{1,0:T(8,128)(2,1)S(1)} %copy-done, f32[8192]{0:T(1024)S(1)} %convert_element_type.29, bf16[128,8192]{1,0:T(8,128)(2,1)S(1)} %copy-done.2, f32[128]{0:T(128)S(1)} %add_rsqrt_fusion), kind=kOutput, calls=%fused_computation | convolution fusion | flops 2168455168 | bytes 19169792 | tf_op jit(solution)/shard_map/dot_general | solution.py:34
  30.5 0.0 reduce-scatter.2.cloned.1.call-update
  30.5 221.3 %all-gather.3.cloned.1.call-done = bf16[1024,8192]{1,0:T(8,128)(2,1)} async-done(((bf16[128,8192]{1,0:T(8,128)(2,1)}), bf16[1024,8192]{1,0:T(8,128)(2,1)}) %all-gather.3.cloned.1.call-update) | async-done | bytes 16777232 | tf_op jit(solution)/shard_map/all_gather | solution.py:24
  251.9 9.1 %reduce_sum.40 = bf16[128,8192]{1,0:T(8,128)(2,1)S(1)} reduce(bf16[8,128,8192]{2,1,0:T(8,128)(2,1)} %bitcast.4, bf16[]{:T(256)} %constant.8.clone.1), dimensions={0}, to_apply=%region_1.0 | reduce | flops 7340032 | bytes 18874370 | tf_op jit(solution)/shard_map/reduce_sum | solution.py:23
  261.0 0.0 copy-start.3
  261.0 0.4 convert_element_type.28
  261.4 1.2 copy-done.3
  262.6 0.0 copy-start.5
  262.6 1.3 multiply_reduce_fusion
  263.9 0.9 multiply_reduce_fusion.1
  264.7 5.8 %psum.7 = f32[1024]{0:T(1024)S(1)} all-reduce(f32[1024]{0:T(1024)S(1)} %get-tuple-element.3), channel_id=1, replica_groups=mesh['dp'=4,'tensor'=8] {'dp'}, use_global_device_ids=true, to_apply=%region_5.0 | all-reduce | flops 1024 | bytes 8192 | tf_op jit(solution)/shard_map/psum | solution.py:33
  270.6 0.0 copy-done.5
  270.6 0.6 multiply_add_fusion
  271.2 0.0 reduce-scatter.2.cloned.1.call-done
  271.2 0.0 copy-start.1
  271.2 10.2 %convert_add_fusion = f32[2048,1024]{1,0:T(8,128)} fusion(f32[2048,1024]{1,0:T(8,128)} %param.10, bf16[2048,1024]{1,0:T(8,128)(2,1)} %reduce-scatter.2.cloned.1.call-done), kind=kLoop, calls=%fused_computation.2 | loop fusion | flops 4194304 | bytes 20971520 | tf_op jit(solution)/shard_map/add | solution.py:37
  281.4 0.0 copy-done.1
  (4 shorter events, 0.0 us)
Async XLA Ops:
  8.0 1.0 copy-start
  8.0 13.7 %copy-start.4 = (bf16[8192]{0:T(1024)(128)(2,1)S(1)}, bf16[8192]{0:T(1024)(128)(2,1)}, u32[]{:S(2)}) copy-start(bf16[8192]{0:T(1024)(128)(2,1)} %param.7) | copy-start | bytes 49156
  8.0 13.7 %copy-start.2 = (bf16[128,8192]{1,0:T(8,128)(2,1)S(1)}, bf16[128,8192]{1,0:T(8,128)(2,1)}, u32[]{:S(2)}) copy-start(bf16[128,8192]{1,0:T(8,128)(2,1)} %param.6) | copy-start | bytes 6291460
  8.0 243.8 %all-gather.3.cloned.1.call-start = ((), (), s32[]{:S(2)}) async-start(), calls=%async_computation.2 | async-start | bytes 18874368 | tf_op jit(solution)/shard_map/all_gather | solution.py:24
  21.7 249.5 %reduce-scatter.2.cloned.1.call-start = ((), (), s32[]{:S(2)}) async-start(), calls=%async_computation.1 | async-start | bytes 20971520 | tf_op jit(solution)/shard_map/reduce_scatter | solution.py:37
  261.0 1.6 copy-start.3
  262.6 8.0 %copy-start.5 = (f32[1024]{0:T(1024)S(1)}, f32[1024]{0:T(1024)}, u32[]{:S(2)}) copy-start(f32[1024]{0:T(1024)} %param.11) | copy-start | bytes 12292
  271.2 10.2 %copy-start.1 = (bf16[128,1024]{1,0:T(8,128)(2,1)S(1)}, bf16[128,1024]{1,0:T(8,128)(2,1)}, u32[]{:S(2)}) copy-start(bf16[128,1024]{1,0:T(8,128)(2,1)} %param.9) | copy-start | bytes 786436
Sparse Core Ops, SparseCore 0:
  21.8 229.9 all-gather.2
Sparse Core Ops, SparseCore 1:
  30.6 127.8 reduce-scatter.1
